TPU v7x, 256 devices: a whole 4x4x8 slice. The times are simulated.
256 devices in a mesh: row: 4 (over x), col: 4 (over y), depth: 16 (over z, core).
Axes of the slice: x: 4, y: 4, z: 8, core: 2. Of those that a mesh axis runs over, the one named last changes fastest.
Arguments:
- tokens: bfloat16 [4096, 4096], P(('col', 'depth'), 'row'), may hold values from -6 to 6
- w_gate: bfloat16 [4096, 14336], P('row', 'col'), may hold values from -0.09375 to 0.09375
- w_up: bfloat16 [4096, 14336], P('row', 'col'), may hold values from -0.09375 to 0.09375
- w_down: bfloat16 [14336, 4096], P('col', 'row'), may hold values from -0.046875 to 0.046875
- cotangent: bfloat16 [4096, 4096], P(('col', 'depth'), 'row'), may hold values from -0.09375 to 0.09375
Outputs:
- mixed: bfloat16 [4096, 4096], P(('col', 'depth'), 'row')
- grad_gate: bfloat16 [4096, 14336], P(('row', 'depth'), 'col')
- grad_up: bfloat16 [4096, 14336], P(('row', 'depth'), 'col')
- grad_down: bfloat16 [14336, 4096], P(('col', 'depth'), 'row')
All inputs are finite; a program needn't handle non-finite values.
Results may differ from a plain program's by a relative error of at most 0.025.
Values may be sent and summed in bfloat16 or wider, within the bound.
A program may use at most 128 MiB of HBM per device.

v0:
```python
import jax
import jax.numpy as jnp
from jax import lax
from jax.sharding import PartitionSpec as P

COLS_CONTRACT = (((1,), (1,)), ((), ()))
ROWS_CONTRACT = (((0,), (0,)), ((), ()))


def copy_for_each(value, axis):
    copies = jnp.broadcast_to(value, (lax.axis_size(axis), *value.shape))
    return lax.all_to_all(copies, axis, split_axis=0, concat_axis=0, tiled=True)


def laid_out(pieces, dim):
    shape = list(pieces.shape[1:])
    shape[dim] *= pieces.shape[0]
    return jnp.moveaxis(pieces, 0, dim).reshape(shape)


def collect(value, axis, dim):
    pieces = copy_for_each(value, axis)
    return laid_out(pieces, dim)


def split_up(value, dim, size):
    shape = value.shape
    pieces = value.reshape(*shape[:dim], size, shape[dim] // size, *shape[dim + 1 :])
    return jnp.moveaxis(pieces, dim, 0)


def sent_and_summed(value, axis, dim):
    pieces = split_up(value, dim, lax.axis_size(axis))
    arrived = lax.all_to_all(pieces, axis, split_axis=0, concat_axis=0, tiled=True)
    return arrived.astype(jnp.float32).sum(axis=0)


def sent_together(arrays, axis, dim, along):
    both = jnp.concatenate(arrays, axis=along)
    whole, at, gathered = (lax.all_gather(both, axis, axis=dim, tiled=True), 0, [])
    for a in arrays:
        gathered.append(lax.slice_in_dim(whole, at, at + a.shape[along], axis=along))
        at += a.shape[along]
    return tuple(gathered)


def in_one_piece(arrays, axis, dim, along):
    ends, at = ([], 0)
    for a in arrays[:-1]:
        at += a.shape[along]
        ends.append(at)
    both = jnp.concatenate(arrays, axis=along)
    return tuple(
        jnp.split(lax.psum_scatter(both, axis, scatter_dimension=dim, tiled=True), ends, axis=along)
    )


def gate_grads(hidden_grad, gate_sum, up_sum):
    sigmoid_gate = jax.nn.sigmoid(gate_sum)
    d_gate = (hidden_grad * up_sum * sigmoid_gate * (1.0 + gate_sum * (1.0 - sigmoid_gate))).astype(
        jnp.bfloat16
    )
    d_up = (hidden_grad * gate_sum * sigmoid_gate).astype(jnp.bfloat16)
    return (d_gate, d_up)


def per_device(tokens, w_gate, w_up, w_down, cotangent):
    hid_width = w_gate.shape[1]
    token_rows = collect(tokens, "col", 0)
    row_piece = token_rows
    joined = lax.psum_scatter(
        jnp.concatenate(
            [
                jnp.dot(row_piece, w_gate, preferred_element_type=jnp.float32),
                jnp.dot(row_piece, w_up, preferred_element_type=jnp.float32),
            ],
            axis=1,
        ).astype(jnp.bfloat16),
        "row",
        scatter_dimension=0,
        tiled=True,
    ).astype(jnp.float32)
    gate_sum = joined[:, :hid_width]
    up_sum = joined[:, hid_width:]
    hidden = (jax.nn.silu(gate_sum) * up_sum).astype(jnp.bfloat16)
    hidden_rows = collect(hidden, "row", 0)
    row_piece = hidden_rows
    mixed = sent_and_summed(
        jnp.dot(row_piece, w_down, preferred_element_type=jnp.float32).astype(jnp.bfloat16),
        "col",
        0,
    ).astype(jnp.bfloat16)
    cot_rows = collect(cotangent, "col", 0)
    row_piece = cot_rows
    hidden_grad = sent_and_summed(
        lax.dot_general(
            row_piece, w_down, COLS_CONTRACT, preferred_element_type=jnp.float32
        ).astype(jnp.bfloat16),
        "row",
        0,
    )
    d_gate, d_up = gate_grads(hidden_grad, gate_sum, up_sum)
    d_gate_rows, d_up_rows = sent_together((d_gate, d_up), "row", 0, 1)
    down_term = lax.dot_general(
        hidden_rows, cot_rows, ROWS_CONTRACT, preferred_element_type=jnp.float32
    )
    gate_term = lax.dot_general(
        token_rows, d_gate_rows, ROWS_CONTRACT, preferred_element_type=jnp.float32
    )
    up_term = lax.dot_general(
        token_rows, d_up_rows, ROWS_CONTRACT, preferred_element_type=jnp.float32
    )
    grad_gate, grad_up, grad_down = (
        *tuple(
            (
                part.astype(jnp.float32)
                for part in in_one_piece(
                    (gate_term.astype(jnp.bfloat16), up_term.astype(jnp.bfloat16)), "depth", 0, 1
                )
            )
        ),
        lax.psum_scatter(
            down_term.astype(jnp.bfloat16), "depth", scatter_dimension=0, tiled=True
        ).astype(jnp.float32),
    )
    return (
        mixed,
        grad_gate.astype(jnp.bfloat16),
        grad_up.astype(jnp.bfloat16),
        grad_down.astype(jnp.bfloat16),
    )


def solution(mesh):
    placed = (
        P(("col", "depth"), "row"),
        P("row", "col"),
        P("row", "col"),
        P("col", "row"),
        P(("col", "depth"), "row"),
    )
    return jax.shard_map(
        per_device,
        mesh=mesh,
        in_specs=placed,
        out_specs=(
            P(("col", "depth"), "row"),
            P(("row", "depth"), "col"),
            P(("row", "depth"), "col"),
            P(("col", "depth"), "row"),
        ),
        check_vma=False,
    )
```

profile of v0, /device:TPU:1, one launch (start us, length us, event | category | flops | bytes accessed | tf_op | source)
XLA Modules:
  0.0 359.1 jit_solution(15815958022471732505)
XLA Ops:
  7.2 0.0 reduce-scatter.6.cloned.1.call-start
  7.2 1.0 broadcast_in_dim.9
  8.2 0.0 slice-start
  8.2 13.7 %all_to_all.25 = bf16[4,64,1024]{2,1,0:T(8,128)(2,1)S(1)} all-to-all(bf16[4,64,1024]{2,1,0:T(8,128)(2,1)S(1)} %broadcast_in_dim.9), channel_id=1, replica_groups=mesh['row'=4,'col'=4,'depth'=16] {'col'}, dimensions={0} | all-to-all | bytes 1048576 | tf_op jit(solution)/shard_map/all_to_all | solution.py:12
  21.9 0.0 slice-start.1
  21.9 5.3 %convolution_convert_fusion.3 = bf16[256,3584]{1,0:T(8,128)(2,1)S(1)} fusion(bf16[256,1024]{1,0:T(8,128)(2,1)S(1)} %bitcast.24, bf16[1024,3584]{1,0:T(8,128)(2,1)} %param.7), kind=kOutput, calls=%fused_computation.7 | convolution fusion | flops 1879965696 | bytes 9699328 | tf_op jit(solution)/shard_map/dot_general | solution.py:75
  27.2 0.0 slice-done
  27.2 0.0 slice-done.1
  27.2 2.1 convolution_convert_fusion.4
  29.3 2.2 pad_maximum_fusion.1
  31.5 0.0 copy-start.1
  31.5 0.0 reduce-scatter.6.cloned.1.call-update
  31.5 0.0 all-gather.2.cloned.1.call-start
  31.6 0.8 copy-done.1
  32.5 10.2 %all_to_all.26 = bf16[4,64,1024]{2,1,0:T(8,128)(2,1)S(1)} all-to-all(bf16[4,64,1024]{2,1,0:T(8,128)(2,1)S(1)} %broadcast_in_dim.11), channel_id=1, replica_groups=mesh['row'=4,'col'=4,'depth'=16] {'col'}, dimensions={0} | all-to-all | bytes 1048576 | tf_op jit(solution)/shard_map/all_to_all | solution.py:12
  42.6 5.6 %convolution_convert_fusion.2 = bf16[256,3584]{1,0:T(8,128)(2,1)S(1)} fusion(bf16[256,1024]{1,0:T(8,128)(2,1)S(1)} %bitcast.30, bf16[3584,1024]{1,0:T(8,128)(2,1)} %param.8), kind=kOutput, calls=%fused_computation.6 | convolution fusion | flops 1879965696 | bytes 9699328 | tf_op jit(solution)/shard_map/dot_general | solution.py:96
  48.2 46.1 %all_to_all.27 = bf16[4,64,3584]{2,1,0:T(8,128)(2,1)S(1)} all-to-all(bf16[4,64,3584]{2,1,0:T(8,128)(2,1)S(1)} %bitcast.29), channel_id=1, replica_groups=mesh['row'=4,'col'=4,'depth'=16] {'row'}, dimensions={0} | all-to-all | bytes 3670016 | tf_op jit(solution)/shard_map/all_to_all | solution.py:34
  94.3 0.3 convert_reduce_fusion
  94.5 3.6 reduce-scatter.6.cloned.1.call-done
  98.1 1.3 convert_element_type.45
  99.4 0.6 multiply_convert_fusion.1
  100.0 1.0 pad_maximum_fusion.2
  101.0 0.0 all-gather.2.cloned.1.call-update
  101.0 0.2 reduce-scatter.10.cloned.1.call-start
  101.3 46.3 %all-gather.2.cloned.1.call-done = bf16[256,7168]{1,0:T(8,128)(2,1)} async-done(((bf16[64,7168]{1,0:T(8,128)(2,1)}), bf16[256,7168]{1,0:T(8,128)(2,1)}) %all-gather.2.cloned.1.call-update) | async-done | bytes 3670032 | tf_op jit(solution)/shard_map/all_gather | solution.py:40
  147.6 0.0 copy-start
  147.6 3.7 %fusion.1 = bf16[1024,3584]{0,1:T(8,128)(2,1)S(1)} fusion(bf16[256,1024]{1,0:T(8,128)(2,1)S(1)} %bitcast.26, bf16[256,7168]{1,0:T(8,128)(2,1)} %all-gather.2.cloned.1.call-done), kind=kOutput, calls=%fused_computation.5 | convolution fusion | flops 1882718208 | bytes 9699328 | tf_op jit(solution)/shard_map/dot_general | solution.py:110
  151.3 0.0 copy-done
  151.3 2.1 fusion
  153.5 21.1 %pad_maximum_fusion = bf16[1024,7168]{0,1:T(8,128)(2,1)} fusion(bf16[1024,3584]{0,1:T(8,128)(2,1)S(1)} %fusion.1, bf16[1024,3584]{0,1:T(8,128)(2,1)S(1)} %fusion), kind=kLoop, calls=%fused_computation | loop fusion | flops 29360128 | bytes 29360128 | tf_op jit(solution)/shard_map/concatenate | solution.py:52
  174.6 19.0 %copy.13 = bf16[1024,7168]{1,0:T(8,128)(2,1)} copy(bf16[1024,7168]{0,1:T(8,128)(2,1)} %pad_maximum_fusion) | data formatting | bytes 29360128
  193.6 0.0 reduce-scatter.10.cloned.1.call-update
  193.6 0.0 reduce-scatter.8.cloned.1.call-start
  193.7 0.1 broadcast_in_dim.10
  193.8 25.3 %all_to_all.28 = bf16[4,64,3584]{2,1,0:T(8,128)(2,1)S(1)} all-to-all(bf16[4,64,3584]{2,1,0:T(8,128)(2,1)S(1)} %broadcast_in_dim.10), channel_id=1, replica_groups=mesh['row'=4,'col'=4,'depth'=16] {'row'}, dimensions={0} | all-to-all | bytes 3670016 | tf_op jit(solution)/shard_map/all_to_all | solution.py:12
  219.1 5.0 %bitcast_convert_fusion = bf16[3584,1024]{1,0:T(8,128)(2,1)} fusion(bf16[4,64,3584]{2,1,0:T(8,128)(2,1)S(1)} %all_to_all.28, bf16[4,64,1024]{2,1,0:T(8,128)(2,1)S(1)} %all_to_all.26), kind=kOutput, calls=%fused_computation.1 | convolution fusion | flops 1882718208 | bytes 9699328 | tf_op jit(solution)/shard_map/dot_general | solution.py:104
  224.1 0.0 reduce-scatter.8.cloned.1.call-update
  224.1 5.3 %convolution_convert_fusion.5 = bf16[256,1024]{1,0:T(8,128)(2,1)S(1)} fusion(bf16[256,3584]{1,0:T(8,128)(2,1)S(1)} %bitcast.28, bf16[3584,1024]{1,0:T(8,128)(2,1)} %param.8), kind=kOutput, calls=%fused_computation.13 | convolution fusion | flops 1879310336 | bytes 9699328 | tf_op jit(solution)/shard_map/dot_general | solution.py:89
  229.4 10.8 %all_to_all.29 = bf16[4,64,1024]{2,1,0:T(8,128)(2,1)S(1)} all-to-all(bf16[4,64,1024]{2,1,0:T(8,128)(2,1)S(1)} %bitcast.31), channel_id=1, replica_groups=mesh['row'=4,'col'=4,'depth'=16] {'col'}, dimensions={0} | all-to-all | bytes 1048576 | tf_op jit(solution)/shard_map/all_to_all | solution.py:34
  240.3 0.7 reduce_sum.21
  241.0 42.1 %reduce-scatter.10.cloned.1.call-done = bf16[64,7168]{1,0:T(8,128)(2,1)} async-done(((bf16[1024,7168]{1,0:T(8,128)(2,1)}), bf16[64,7168]{1,0:T(8,128)(2,1)}) %reduce-scatter.10.cloned.1.call-update) | async-done | bytes 917520
  283.1 2.1 fusion.4
  285.3 67.2 %reduce-scatter.8.cloned.1.call-done = bf16[224,1024]{1,0:T(8,128)(2,1)} async-done(((bf16[3584,1024]{1,0:T(8,128)(2,1)}), bf16[224,1024]{1,0:T(8,128)(2,1)}) %reduce-scatter.8.cloned.1.call-update) | async-done | bytes 458768 | tf_op jit(solution)/shard_map/reduce_scatter | solution.py:122
  (2 shorter events, 0.0 us)
Async XLA Ops:
  7.2 90.9 %reduce-scatter.6.cloned.1.call-start = ((), (), s32[]{:S(2)}) async-start(), calls=%async_computation.8 | async-start | bytes 4587520 | tf_op jit(solution)/shard_map/reduce_scatter | solution.py:71
  8.2 19.0 %slice-start = ((s8[7340032]{0:T(1024)(128)(4,1)}), s8[4194304]{0:T(1024)(128)(4,1)S(1)}, s32[]{:S(2)}) async-start(s8[7340032]{0:T(1024)(128)(4,1)} %bitcast.32), calls=%async_computation.12 | async-start | bytes 8388608
  21.9 5.3 %slice-start.1 = ((s8[7340032]{0:T(1024)(128)(4,1)}), s8[3145728]{0:T(1024)(128)(4,1)S(1)}, s32[]{:S(2)}) async-start(s8[7340032]{0:T(1024)(128)(4,1)} %bitcast.32), calls=%async_computation.13 | async-start | bytes 6291456
  31.5 0.9 copy-start.1
  31.5 116.1 %all-gather.2.cloned.1.call-start = ((), (), s32[]{:S(2)}) async-start(), calls=%async_computation.9 | async-start | bytes 4587520 | tf_op jit(solution)/shard_map/all_gather | solution.py:40
  101.0 182.1 %reduce-scatter.10.cloned.1.call-start = ((), (), s32[]{:S(2)}) async-start(), calls=%async_computation.11 | async-start | bytes 15597568
  147.6 3.8 %copy-start = (bf16[256,7168]{1,0:T(8,128)(2,1)S(1)}, bf16[256,7168]{1,0:T(8,128)(2,1)}, u32[]{:S(2)}) copy-start(bf16[256,7168]{1,0:T(8,128)(2,1)} %all-gather.2.cloned.1.call-done) | copy-start | bytes 11010052
  193.6 158.9 %reduce-scatter.8.cloned.1.call-start = ((), (), s32[]{:S(2)}) async-start(), calls=%async_computation.10 | async-start | bytes 7798784 | tf_op jit(solution)/shard_map/reduce_scatter | solution.py:122
Sparse Core Ops, SparseCore 0:
  31.7 66.4 reduce-scatter.5
  101.2 46.3 all-gather.1
  193.7 89.3 reduce-scatter.9
  286.1 66.3 reduce-scatter.7
where the time goes:
time: 362 us; the launch traced here: 359 us
  waiting for transfers between devices  159 us (44%)
  blocking collectives  106 us (29%)
  matrix products  29.2 us (8%)
  other arithmetic  27.2 us (8%)
  local copies, waits for them, and re-layouts  23.1 us (6%)
  between operations  13.9 us (4%)
    reduce_scatter x1, waiting for transfers between devices, per_device(): lax.psum_scatter(down_term.astype(jnp.bfloat16), 'depth', scatter_dimensi...  67.2 us
    all_to_all x2, blocking collectives, sent_and_summed(): lax.all_to_all(pieces, axis, split_axis=0, concat_axis=0, tiled=True)  56.9 us
    all_to_all x3, blocking collectives, copy_for_each(): return lax.all_to_all(copies, axis, split_axis=0, concat_axis=0, tiled=True)  49.1 us
    all_gather x1, waiting for transfers between devices, sent_together(): lax.all_gather(both, axis, axis=dim, tiled=True)  46.3 us
    unnamed x5, waiting for transfers between devices  42.2 us
    concatenate x1, other arithmetic, in_one_piece(): both = jnp.concatenate(arrays, axis=along)  21.1 us
    unnamed x9, local copies, waits for them, and re-layouts  19.8 us
  transfers between devices with their start and end apart: 4, of which 4 were waited for; matrix products, arithmetic and copies ran while one was open for 5% of the time, Pallas kernels for 0%

commit v1 on v0

v1 whole, which is shorter than its diff:
```python
import jax
import jax.numpy as jnp
from jax import lax
from jax.experimental import pallas as pl
from jax.experimental.pallas import tpu as pltpu
from jax.sharding import PartitionSpec as P

MESH = pl.DeviceIdType.MESH
BF, F32 = jnp.bfloat16, jnp.float32
TD, FW, HW = 64, 1024, 3584
NY, NZ = 4, 8
CW = 128
HC = HW // 2
NC = HC // CW
TK = 2 * NY * TD
OW = TK // 4
HF = OW // 2
PIECE = HC // 8
SL, PS = 4, 6

TICK = {"A": 0, "RS2": 1, "AG1": 2, "AG2": 3, "E": 4, "Z1": 6, "Z2": 7, "Z3": 8, "Z4": 9, "Z5": 10, "Z6": 11, "FIN": 12}
ORDER = ["FIN", "Z6", "Z5", "Z4", "Z3", "Z2", "Z1", "AG2", "AG1", "RS2", "A", "E"]


def remote(src, dst, ssem, rsem, **dev):
    return pltpu.make_async_remote_copy(
        src_ref=src, dst_ref=dst, send_sem=ssem, recv_sem=rsem, device_id=dev, device_id_type=MESH
    )


def mod(a, n):
    return lax.rem(a + n, n)


def rows(start, size):
    return pl.ds(pl.multiple_of(start, size), size)


def kernel(
    tok, wg, wu, wd, cot, o_mix, o_gate, o_up, o_down,
    T, C, TT, CT, WGU, WD, PX, R1, R2, G, PZ, ZB, ACC, XS, OGU, GDT, OGD, MS, MR, MYS, MYR, OM,
    s_in, s_w, s_ag, r_ag, s_fw, s_x1, r_x1, s_x2, r_x2, s_g1, r_g1, s_g2, r_g2, s_z, r_z,
    s_xs, r_xs, s_gd, r_gd, s_m, r_m, s_my, r_my, s_out,
):
    r, y, d = lax.axis_index("row"), lax.axis_index("col"), lax.axis_index("depth")
    z, k = lax.div(d, 2), lax.rem(d, 2)
    right, left = mod(r + 1, 4), mod(r + 3, 4)
    opp = mod(r + 2, 4)
    zup = 2 * mod(z + 1, NZ) + k
    zdn = 2 * mod(z + NZ - 1, NZ) + k
    mate = 2 * z + (1 - k)
    own = 4 * k + y

    in_t = pltpu.make_async_copy(tok, T.at[rows(own * TD, TD), :], s_in.at[0])
    in_c = pltpu.make_async_copy(cot, C.at[rows(own * TD, TD), :], s_in.at[1])
    in_t.start()
    in_c.start()

    def weight_copies(j):
        at = pl.ds(pl.multiple_of(k * HC + j * CW, CW), CW)
        return (
            pltpu.make_async_copy(wg.at[:, at], WGU.at[j, :, pl.ds(0, CW)], s_w.at[0, j]),
            pltpu.make_async_copy(wu.at[:, at], WGU.at[j, :, pl.ds(CW, CW)], s_w.at[1, j]),
            pltpu.make_async_copy(wd.at[at, :], WD.at[j], s_w.at[2, j]),
        )

    barrier = pltpu.get_barrier_semaphore()
    for other in (right, left):
        pl.semaphore_signal(barrier, inc=1, device_id={"row": other}, device_id_type=MESH)
    for dy in range(1, 4):
        pl.semaphore_signal(barrier, inc=1, device_id={"col": mod(y + dy, 4)}, device_id_type=MESH)
    for dd in range(1, 16):
        pl.semaphore_signal(barrier, inc=1, device_id={"depth": mod(d + dd, 16)}, device_id_type=MESH)

    @pl.loop(0, NC)
    def _(j):
        for c in weight_copies(j):
            c.start()

    ACC[...] = jnp.zeros_like(ACC)
    pl.semaphore_wait(barrier, 20)

    def block_of(a, b):
        return (T, C)[a].at[rows(b * TD, TD), :]

    for a, mine in ((0, in_t), (1, in_c)):
        mine.wait()
        for dy in (1, 3, 2):
            remote(block_of(a, own), block_of(a, own), s_ag.at[a, dy], r_ag.at[a, own], col=mod(y + dy, 4)).start()
        remote(block_of(a, own), block_of(a, own), s_ag.at[a, 0], r_ag.at[a, own], depth=mate).start()
    for a in (0, 1):
        for dy in (1, 3, 2):
            b = 4 * k + mod(y + dy, 4)
            remote(block_of(a, b), block_of(a, b), s_fw.at[a, dy - 1], r_ag.at[a, b], depth=mate).wait_recv()
            remote(block_of(a, b), block_of(a, b), s_fw.at[a, dy - 1], r_ag.at[a, b], depth=mate).start()
    for a in (0, 1):
        for yy in range(4):
            b = 4 * (1 - k) + yy
            remote(block_of(a, b), block_of(a, b), s_fw.at[a, 0], r_ag.at[a, b], depth=mate).wait_recv()
    for a in (0, 1):
        for dy in range(4):
            remote(block_of(a, own), block_of(a, own), s_ag.at[a, dy], r_ag.at[a, own], depth=mate).wait_send()
        for dy in (1, 3, 2):
            b = 4 * k + mod(y + dy, 4)
            remote(block_of(a, b), block_of(a, b), s_fw.at[a, dy - 1], r_ag.at[a, b], depth=mate).wait_send()

    def xto(di):
        return {"row": (right, left)[di]}

    def x1_copy(j, di):
        sl = lax.rem(j, SL)
        src = PX.at[sl, :, rows(opp * OW + di * HF, HF), :]
        return remote(src, R1.at[sl, di], s_x1.at[di, sl], r_x1.at[di, sl], **xto(di))

    def x2_copy(j, di):
        sl = lax.rem(j, SL)
        src = PX.at[sl, :, rows((right, left)[di] * OW, OW), :]
        return remote(src, R2.at[sl, di], s_x2.at[di, sl], r_x2.at[di, sl], **xto(di))

    def g1_copy(j, di, owner):
        sl = lax.rem(j, SL)
        at = G.at[sl, :, rows(owner * OW, OW), :]
        return remote(at, at, s_g1.at[di, sl], r_g1.at[di, sl], **xto(di))

    def g2_copy(j, di, owner):
        sl = lax.rem(j, SL)
        at = G.at[sl, :, rows(owner * OW + di * HF, HF), :]
        return remote(at, at, s_g2.at[di, sl], r_g2.at[di, sl], **xto(di))

    def zrow(di, s):
        q = mod(z - 1 - s + NZ, NZ) if di == 0 else mod(z + 1 + s, NZ)
        return rows(q * 128 + di * 64, 64)

    def z_copy(j, di, s):
        sl = lax.rem(j, SL)
        if s == 0:
            src = PZ.at[lax.rem(j, PS), :, zrow(di, 0), :]
        else:
            src = ZB.at[di, s - 1, sl]
        return remote(src, ZB.at[di, s, sl], s_z.at[di, s, sl], r_z.at[di, s, sl], depth=(zup, zdn)[di])

    def stage_a(j):
        sl = lax.rem(j, SL)
        for c in weight_copies(j):
            c.wait()
        for m in range(2):
            at = pl.ds(m * 256, 256)
            gu = jnp.dot(T[at, :], WGU[j], preferred_element_type=F32)
            h = lax.dot_general(C[at, :], WD[j], (((1,), (1,)), ((), ())), preferred_element_type=F32)
            PX[sl, 0, at, :] = gu[:, :CW].astype(BF)
            PX[sl, 1, at, :] = gu[:, CW:].astype(BF)
            PX[sl, 2, at, :] = h.astype(BF)
        for di in (0, 1):
            x1_copy(j, di).start()

    def stage_rs2(j):
        sl = lax.rem(j, SL)
        for di in (0, 1):
            x1_copy(j, di).wait_recv()
            at = rows((right, left)[di] * OW + di * HF, HF)
            PX[sl, :, at, :] = (PX[sl, :, at, :].astype(F32) + R1[sl, di].astype(F32)).astype(BF)
            x2_copy(j, di).start()

    def stage_ag1(j):
        sl = lax.rem(j, SL)
        for di in (0, 1):
            x1_copy(j, di).wait_send()
        for di in (0, 1):
            x2_copy(j, di).wait_recv()
        at = rows(r * OW, OW)
        total = PX[sl, :, at, :].astype(F32) + R2[sl, 0].astype(F32) + R2[sl, 1].astype(F32)
        gate, up, hg = total[0], total[1], total[2]
        sig = jax.nn.sigmoid(gate)
        G[sl, 0, at, :] = (gate * sig * up).astype(BF)
        G[sl, 1, at, :] = (hg * up * sig * (1.0 + gate * (1.0 - sig))).astype(BF)
        G[sl, 2, at, :] = (hg * gate * sig).astype(BF)
        for di in (0, 1):
            g1_copy(j, di, r).start()

    def stage_ag2(j):
        for di in (0, 1):
            frm = (left, right)[di]
            g1_copy(j, di, frm).wait_recv()
            g2_copy(j, di, frm).start()

    def stage_e(j):
        sl, ps = lax.rem(j, SL), lax.rem(j, PS)
        for di in (0, 1):
            x2_copy(j, di).wait_send()
            g1_copy(j, di, r).wait_send()
        for di in (0, 1):
            g2_copy(j, di, opp).wait_recv()
        hid = G[sl, 0]
        dgu = jnp.concatenate([G[sl, 1], G[sl, 2]], axis=1)
        for m in range(4):
            at = pl.ds(m * 256, 256)
            gu = jnp.dot(TT[at, :], dgu, preferred_element_type=F32)
            PZ[ps, 0, at, :] = gu[:, :CW].astype(BF)
            PZ[ps, 1, at, :] = gu[:, CW:].astype(BF)
            PZ[ps, 2, at, :] = jnp.dot(CT[at, :], hid, preferred_element_type=F32).astype(BF)
        for di in (0, 1):
            z_copy(j, di, 0).start()
        for m in range(4):
            at = pl.ds(m * 128, 128)
            ACC[at, :] += jnp.dot(G[sl, 0, at, :], WD[j], preferred_element_type=F32)

    def stage_z(s):
        def run(j):
            sl, ps = lax.rem(j, SL), lax.rem(j, PS)
            if s == 1:
                for di in (0, 1):
                    g2_copy(j, di, (left, right)[di]).wait_send()
            else:
                for di in (0, 1):
                    z_copy(j, di, s - 2).wait_send()
            for di in (0, 1):
                z_copy(j, di, s - 1).wait_recv()
                part = PZ[ps, :, zrow(di, s), :].astype(F32)
                ZB[di, s - 1, sl] = (ZB[di, s - 1, sl].astype(F32) + part).astype(BF)
                z_copy(j, di, s).start()

        return run

    def swap_copy(j):
        at = OGU.at[:, :, pl.ds(pl.multiple_of(k * HC + j * CW, CW), CW)]
        return remote(XS.at[j], at, s_xs.at[j], r_xs.at[j], depth=mate)

    def swap_in(j):
        at = OGU.at[:, :, pl.ds(pl.multiple_of((1 - k) * HC + j * CW, CW), CW)]
        return remote(XS.at[j], at, s_xs.at[j], r_xs.at[j], depth=mate)

    def piece_src(m):
        return GDT.at[rows(m * PIECE, 32) if False else pl.ds(pl.multiple_of(m * PIECE, 32), PIECE), :]

    def piece_dst(zz):
        return OGD.at[:, rows(zz * 128, 128)]

    def piece_copy(m):
        return remote(piece_src(m), piece_dst(z), s_gd.at[m], r_gd.at[z], depth=8 * k + m)

    def piece_local(m):
        return pltpu.make_async_copy(piece_src(m), piece_dst(z), r_gd.at[z])

    def stage_fin(j):
        sl, ps = lax.rem(j, SL), lax.rem(j, PS)
        sums = []
        for di in (0, 1):
            for s in (5, 6):
                z_copy(j, di, s).wait_send()
        for di in (0, 1):
            z_copy(j, di, 6).wait_recv()
            part = PZ[ps, :, rows(z * 128 + di * 64, 64), :].astype(F32)
            sums.append(ZB[di, 6, sl].astype(F32) + part)
        lo, hi = sums
        first = k == 0
        at = pl.ds(pl.multiple_of(k * HC + j * CW, CW), CW)
        OGU[:, :, at] = jnp.where(first, lo[:2], hi[:2]).astype(BF)
        XS[j] = jnp.where(first, hi[:2], lo[:2]).astype(BF)
        swap_copy(j).start()
        down = jnp.concatenate([lo[2], hi[2]], axis=0)
        GDT[rows(j * CW, CW), :] = down.T.astype(BF)
        m = lax.div(4 * j, 7)

        @pl.when(lax.div(4 * (j + 1), 7) > m)
        def _():
            to_self = 8 * k + m == d

            @pl.when(to_self)
            def _():
                piece_local(m).start()

            @pl.when(jnp.logical_not(to_self))
            def _():
                piece_copy(m).start()

    def mate_copy():
        return remote(MS, MR, s_m.at[0], r_m.at[0], depth=mate)

    def col_copy(dy):
        return remote(MYS.at[dy], MYR.at[dy], s_my.at[dy], r_my.at[dy], col=mod(y + dy, 4))

    def mix1():
        MS[...] = ACC[rows((1 - k) * 256, 256), :].astype(BF)
        mate_copy().start()

    def mix2():
        mate_copy().wait()
        for dy in (1, 3, 2):
            yy = mod(y + dy, 4)
            total = ACC[rows(k * 256 + yy * TD, TD), :] + MR[rows(yy * TD, TD), :].astype(F32)
            MYS[dy] = total.astype(BF)
            col_copy(dy).start()

    def mix3():
        total = ACC[rows(k * 256 + y * TD, TD), :] + MR[rows(y * TD, TD), :].astype(F32)
        for dy in (1, 3, 2):
            col_copy(dy).wait()
            total = total + MYR[dy].astype(F32)
        OM[...] = total.astype(BF)
        pltpu.make_async_copy(OM, o_mix, s_out.at[0]).start()

    TT[...] = T[...].T
    CT[...] = C[...].T

    stages = {"A": stage_a, "RS2": stage_rs2, "AG1": stage_ag1, "AG2": stage_ag2, "E": stage_e, "FIN": stage_fin}
    for s in range(1, 7):
        stages[f"Z{s}"] = stage_z(s)
    last_e = NC - 1 + TICK["E"] // 2

    @pl.loop(0, NC + TICK["FIN"] // 2)
    def _(i):
        for parity in (0, 1):
            for name in ORDER:
                if TICK[name] % 2 != parity:
                    continue
                j = i - TICK[name] // 2

                @pl.when(jnp.logical_and(j >= 0, j < NC))
                def _(name=name, j=j):
                    stages[name](j)

            if parity == 1:
                for n, step in enumerate((mix1, mix2, mix3)):
                    pl.when(i == last_e + n)(step)

    outs = []
    for j in range(NC):
        swap_in(j).wait_recv()
    for n, o in ((0, o_gate), (1, o_up)):
        outs.append(pltpu.make_async_copy(OGU.at[n], o, s_out.at[1 + n]))
        outs[-1].start()
    has_self = lax.div(d, 8) == k
    for zz in range(NZ):
        local = jnp.logical_and(has_self, z == zz)

        @pl.when(local)
        def _(zz=zz):
            pltpu.make_async_copy(piece_src(0), piece_dst(zz), r_gd.at[zz]).wait()

        @pl.when(jnp.logical_not(local))
        def _(zz=zz):
            remote(piece_src(0), piece_dst(zz), s_gd.at[0], r_gd.at[zz], depth=mate).wait_recv()

    outs.append(pltpu.make_async_copy(OGD, o_down, s_out.at[3]))
    outs[-1].start()
    for j in range(NC):
        swap_copy(j).wait_send()
    for m in range(8):

        @pl.when(8 * k + m != d)
        def _(m=m):
            piece_copy(m).wait_send()

    pltpu.make_async_copy(OM, o_mix, s_out.at[0]).wait()
    for o in outs:
        o.wait()


def per_device(tokens, w_gate, w_up, w_down, cotangent):
    dma = pltpu.SemaphoreType.DMA
    scratch = [
        pltpu.VMEM((TK, FW), BF),
        pltpu.VMEM((TK, FW), BF),
        pltpu.VMEM((FW, TK), BF),
        pltpu.VMEM((FW, TK), BF),
        pltpu.VMEM((NC, FW, 2 * CW), BF),
        pltpu.VMEM((NC, CW, FW), BF),
        pltpu.VMEM((SL, 3, TK, CW), BF),
        pltpu.VMEM((SL, 2, 3, HF, CW), BF),
        pltpu.VMEM((SL, 2, 3, OW, CW), BF),
        pltpu.VMEM((SL, 3, TK, CW), BF),
        pltpu.VMEM((PS, 3, FW, CW), BF),
        pltpu.VMEM((2, 7, SL, 3, 64, CW), BF),
        pltpu.VMEM((TK, FW), F32),
        pltpu.VMEM((NC, 2, 64, CW), BF),
        pltpu.VMEM((2, 64, HW), BF),
        pltpu.VMEM((HC, 128), BF),
        pltpu.VMEM((PIECE, FW), BF),
        pltpu.VMEM((256, FW), BF),
        pltpu.VMEM((256, FW), BF),
        pltpu.VMEM((4, TD, FW), BF),
        pltpu.VMEM((4, TD, FW), BF),
        pltpu.VMEM((TD, FW), BF),
        dma((2,)), dma((3, NC)),
        dma((2, 4)), dma((2, 8)), dma((2, 3)),
        dma((2, SL)), dma((2, SL)), dma((2, SL)), dma((2, SL)),
        dma((2, SL)), dma((2, SL)), dma((2, SL)), dma((2, SL)),
        dma((2, 7, SL)), dma((2, 7, SL)),
        dma((NC,)), dma((NC,)), dma((8,)), dma((8,)),
        dma((1,)), dma((1,)), dma((4,)), dma((4,)), dma((4,)),
    ]
    anyspec = pl.BlockSpec(memory_space=pl.ANY)
    return pl.pallas_call(
        kernel,
        out_shape=(
            jax.ShapeDtypeStruct((TD, FW), BF),
            jax.ShapeDtypeStruct((FW // 16, HW), BF),
            jax.ShapeDtypeStruct((FW // 16, HW), BF),
            jax.ShapeDtypeStruct((HW // 16, FW), BF),
        ),
        in_specs=[anyspec] * 5,
        out_specs=(anyspec,) * 4,
        scratch_shapes=scratch,
        compiler_params=pltpu.CompilerParams(
            collective_id=0, has_side_effects=True, vmem_limit_bytes=58 * 1024 * 1024
        ),
    )(tokens, w_gate, w_up, w_down, cotangent)


def solution(mesh):
    tok, grad = P(("col", "depth"), "row"), P(("row", "depth"), "col")
    return jax.shard_map(
        per_device,
        mesh=mesh,
        in_specs=(tok, P("row", "col"), P("row", "col"), P("col", "row"), tok),
        out_specs=(tok, grad, grad, P(("col", "depth"), "row")),
        check_vma=False,
    )
```

time: 362 us -> 222 us (0.61)
  Pallas kernels: 0 us -> 212 us
  waiting for transfers between devices: 159 us -> 0 us
  blocking collectives: 106 us -> 0 us
  matrix products: 29.2 us -> 0 us
  other arithmetic: 27.2 us -> 0 us
  local copies, waits for them, and re-layouts: 23.1 us -> 7.01 us
  between operations: 13.9 us -> 0.64 us
    pallas_call x0 -> x1, Pallas kernels: none -> 212 us  [per_device(): pl.pallas_call(kernel, out_shape=(jax.ShapeDtypeStruct((TD, FW), BF), jax...]
    all_to_all x5 -> x0, blocking collectives: 106 us -> none  [the longest x2 56.9 us: sent_and_summed(): lax.all_to_all(pieces, axis, split_axis=0, concat_axis=0, tiled=True)]
    reduce_scatter x2 -> x0, waiting for transfers between devices: 70.8 us -> none  [the longest x1 67.2 us: per_device(): lax.psum_scatter(down_term.astype(jnp.bfloat16), 'depth', scatter_dimensi...]
    all_gather x1 -> x0, waiting for transfers between devices: 46.3 us -> none  [sent_together(): lax.all_gather(both, axis, axis=dim, tiled=True)]
    unnamed x5 -> x0, waiting for transfers between devices: 42.2 us -> none
    dot_general x7 -> x0, matrix products: 29.2 us -> none  [the longest x1 5.57 us: per_device(): lax.dot_general(row_piece, w_down, COLS_CONTRACT, preferred_element_type=...]
    concatenate x3 -> x0, other arithmetic: 24.3 us -> none  [the longest x1 21.1 us: in_one_piece(): both = jnp.concatenate(arrays, axis=along)]
    unnamed x9 -> x4, local copies, waits for them, and re-layouts: 19.8 us -> 7.01 us
  transfers between devices with their start and end apart: 4 -> 0, of which waited for: 4 -> 0; matrix products, arithmetic and copies ran while one was open for 5% -> 0% of each run, Pallas kernels for 0% -> 0%
where the time goes in v1:
time: 222 us; the launch traced here: 220 us
  Pallas kernels  212 us (95%)
  local copies, waits for them, and re-layouts  7.01 us (3%)
    pallas_call x1, Pallas kernels, per_device(): pl.pallas_call(kernel, out_shape=(jax.ShapeDtypeStruct((TD, FW), BF), jax...  212 us
    unnamed x4, local copies, waits for them, and re-layouts  7.01 us

profile of v1, /device:TPU:1, one launch (start us, length us, event | category | flops | bytes accessed | tf_op | source)
XLA Modules:
  0.0 220.0 jit_solution(10358253265721717428)
XLA Ops:
  0.6 212.4 %shard_map.84 = (bf16[64,1024]{1,0:T(8,128)(2,1)}, bf16[64,3584]{1,0:T(8,128)(2,1)}, bf16[64,3584]{1,0:T(8,128)(2,1)}, bf16[224,1024]{1,0:T(8,128)(2,1)}) custom-call(bf16[64,1024]{1,0:T(8,128)(2,1)} %tok.1, bf16[1024,3584]{1,0:T(8,128)(2,1)} %wg.1, bf16[1024,3584]{1,0:T(8,128)(2,1)} %wu.1, bf16[3584,1024]{1,0:T(8,128)(2,1)} %wd.1, bf16[64,1024]{1,0:T(8,128)(2,1)} %cot.1), custom_call_target="tpu_custom_call" | custom-call | tf_op jit(solution)/shard_map/pallas_call | solution.py:393
  213.0 1.6 copy.13
  214.6 1.8 copy.14
  216.4 1.8 copy.15
  218.2 1.8 copy.16

commit v2 on v1

v2 whole, which is shorter than its diff:
```python
import jax
import jax.numpy as jnp
from jax import lax
from jax.experimental import pallas as pl
from jax.experimental.pallas import tpu as pltpu
from jax.sharding import PartitionSpec as P

MESH = pl.DeviceIdType.MESH
BF, F32 = jnp.bfloat16, jnp.float32
TD, FW, HW = 64, 1024, 3584
NY, NZ = 4, 8
CW = 128
HC = HW // 2
NC = HC // CW
TK = 2 * NY * TD
OW = TK // 4
HF = OW // 2
SL, ZS, PS = 6, 6, 12
ST = CW // NZ

PT = 3
TICK = {"A": 0, "RS2": 2, "AG1": 5, "AG2": 8, "E": 10, "Z1": 13, "Z2": 15, "Z3": 17, "Z4": 19, "Z5": 21, "Z6": 23, "FIN": 25}
ORDER = ["FIN", "Z6", "Z5", "Z4", "Z3", "Z2", "Z1", "AG2", "AG1", "RS2", "A", "E"]


def remote(src, dst, ssem, rsem, **dev):
    return pltpu.make_async_remote_copy(
        src_ref=src, dst_ref=dst, send_sem=ssem, recv_sem=rsem, device_id=dev, device_id_type=MESH
    )


def mod(a, n):
    return lax.rem(a + n, n)


def rows(start, size):
    return pl.ds(pl.multiple_of(start, size), size)


def kernel(
    tok, wg, wu, wd, cot, o_mix, o_gate, o_up, o_down,
    T, C, TT, WG, WU, WC, WD, PX, R1, R2, G, PZ, ZB, ACC, XS, XR, OGU, OGB, OGD, MS, MR, MYS, MYR, OM,
    s_in, s_w, s_wd, s_ag, r_ag, s_fw, s_rl, r_rl, s_x1, r_x1, s_x2, r_x2, s_g1, r_g1, s_g2, r_g2, s_z, r_z,
    s_xs, r_xs, s_m, r_m, s_my, r_my, s_out,
):
    r, y, d = lax.axis_index("row"), lax.axis_index("col"), lax.axis_index("depth")
    z, k = lax.div(d, 2), lax.rem(d, 2)
    right, left = mod(r + 1, 4), mod(r + 3, 4)
    opp = mod(r + 2, 4)
    zup = 2 * mod(z + 1, NZ) + k
    zdn = 2 * mod(z + NZ - 1, NZ) + k
    mate = 2 * z + (1 - k)
    own = 4 * k + y

    in_t = pltpu.make_async_copy(tok, T.at[rows(own * TD, TD), :], s_in.at[0])
    in_c = pltpu.make_async_copy(cot, C.at[rows(own * TD, TD), :], s_in.at[1])
    in_t.start()
    in_c.start()

    def start_down(j):
        for zz in range(NZ):
            src = wd.at[pl.ds(pl.multiple_of(448 * zz + 224 * k + ST * j, ST), ST), :]
            to = lax.rem(16 * (6 * k + j + 4 * (zz % 2) + zz // 2), CW)
            pltpu.make_async_copy(src, WD.at[j, rows(to, ST), :], s_wd.at[j]).start()

    def wide_copy(n, q):
        at = pl.ds(q * 256, 256)
        return pltpu.make_async_copy((wg, wu)[n].at[at, :], (WG, WU)[n].at[at, :], s_w.at[n])

    barrier = pltpu.get_barrier_semaphore()
    for other in (right, left):
        pl.semaphore_signal(barrier, inc=1, device_id={"row": other}, device_id_type=MESH)
    for dy in range(1, 4):
        pl.semaphore_signal(barrier, inc=1, device_id={"col": mod(y + dy, 4)}, device_id_type=MESH)
    for dd in range(1, 16):
        pl.semaphore_signal(barrier, inc=1, device_id={"depth": mod(d + dd, 16)}, device_id_type=MESH)

    for n in (0, 1):
        for q in range(4):
            wide_copy(n, q).start()
    pl.loop(0, NC)(start_down)
    ACC[...] = jnp.zeros_like(ACC)
    pl.semaphore_wait(barrier, 20)

    def block_of(a, b):
        return (T, C)[a].at[rows(b * TD, TD), :]

    yto = (mod(y + 1, 4), mod(y + 3, 4))
    yop = 4 * k + mod(y + 2, 4)

    def own_copy(a, di):
        dev = {"depth": mate} if di == 2 else {"col": yto[di]}
        return remote(block_of(a, own), block_of(a, own), s_ag.at[a, di], r_ag.at[a, own], **dev)

    def relay_copy(a, di, b):
        at = (T, C)[a].at[rows(b * TD + di * (TD // 2), TD // 2), :]
        return remote(at, at, s_rl.at[a, di], r_rl.at[a, di], col=yto[di])

    def mate_block(a, n, b):
        return remote(block_of(a, b), block_of(a, b), s_fw.at[a, n], r_ag.at[a, b], depth=mate)

    for a, mine in ((0, in_t), (1, in_c)):
        mine.wait()
        for di in range(3):
            own_copy(a, di).start()
    for a in (0, 1):
        for di in (0, 1):
            b = 4 * k + yto[1 - di]
            mate_block(a, di, b).wait_recv()
            relay_copy(a, di, b).start()
            mate_block(a, di, b).start()
    for a in (0, 1):
        for di in (0, 1):
            relay_copy(a, di, yop).wait_recv()
        mate_block(a, 2, yop).start()
    for a in (0, 1):
        for yy in range(4):
            mate_block(a, 0, 4 * (1 - k) + yy).wait_recv()

    def xto(di):
        return {"row": (right, left)[di]}

    def x1_copy(j, di):
        sl = lax.rem(j, SL)
        src = PX.at[sl, :, rows(opp * OW + di * HF, HF), :]
        return remote(src, R1.at[sl, di], s_x1.at[di, sl], r_x1.at[di, sl], **xto(di))

    def x2_copy(j, di):
        sl = lax.rem(j, SL)
        src = PX.at[sl, :, rows((right, left)[di] * OW, OW), :]
        return remote(src, R2.at[sl, di], s_x2.at[di, sl], r_x2.at[di, sl], **xto(di))

    def g1_copy(j, di, owner):
        sl = lax.rem(j, SL)
        at = G.at[sl, :, rows(owner * OW, OW), :]
        return remote(at, at, s_g1.at[di, sl], r_g1.at[di, sl], **xto(di))

    def g2_copy(j, di, owner):
        sl = lax.rem(j, SL)
        at = G.at[sl, :, rows(owner * OW + di * HF, HF), :]
        return remote(at, at, s_g2.at[di, sl], r_g2.at[di, sl], **xto(di))

    def zrow(di, s):
        q = mod(z - 1 - s + NZ, NZ) if di == 0 else mod(z + 1 + s, NZ)
        return rows(q * 128 + di * 64, 64)

    def z_copy(j, di, s):
        sl = lax.rem(j, ZS)
        if s == 0:
            src = PZ.at[lax.rem(j, PS), :, zrow(di, 0), :]
        else:
            src = ZB.at[di, s - 1, sl]
        return remote(src, ZB.at[di, s, sl], s_z.at[di, s, sl], r_z.at[di, s, sl], depth=(zup, zdn)[di])

    def lane_block(kk, j, zz):
        return rows(lax.div(448 * zz + 224 * kk + ST * j, CW) * CW, CW)

    def strip_at(j):
        lane = lax.broadcasted_iota(jnp.int32, (128, CW), 1)
        u = lax.rem(lax.div(lane, ST) + 16 - lax.rem(6 * k + j, 8), 8)
        return 2 * lax.rem(u, 4) + lax.div(u, 4)

    def stage_a(j):
        sl = lax.rem(j, SL)
        pltpu.make_async_copy(wd.at[pl.ds(0, CW), :], WD.at[j], s_wd.at[j]).wait()

        @pl.when(j == 0)
        def _():
            for n, (w, buf) in enumerate(((wg, WG), (wu, WU))):
                pltpu.make_async_copy(w, buf, s_w.at[n]).wait()

        which = strip_at(j)
        for n, buf in enumerate((WG, WU)):
            for q in range(8):
                at = pl.ds(q * 128, 128)
                got = buf[at, lane_block(k, j, 0)]
                for zz in range(1, NZ):
                    part = buf[at, lane_block(k, j, zz)]
                    if zz // 2:
                        part = pltpu.roll(part, ST * (zz // 2), 1)
                    got = jnp.where(which == zz, part, got)
                WC[at, n * CW : (n + 1) * CW] = got
        for m in range(2):
            at = pl.ds(m * 256, 256)
            gu = jnp.dot(T[at, :], WC[...], preferred_element_type=F32)
            h = lax.dot_general(C[at, :], WD[j], (((1,), (1,)), ((), ())), preferred_element_type=F32)
            PX[sl, 0, at, :] = gu[:, :CW].astype(BF)
            PX[sl, 1, at, :] = gu[:, CW:].astype(BF)
            PX[sl, 2, at, :] = h.astype(BF)
        for di in (0, 1):
            x1_copy(j, di).start()

    def stage_rs2(j):
        sl = lax.rem(j, SL)
        for di in (0, 1):
            x1_copy(j, di).wait_recv()
            at = rows((right, left)[di] * OW + di * HF, HF)
            PX[sl, :, at, :] = (PX[sl, :, at, :].astype(F32) + R1[sl, di].astype(F32)).astype(BF)
            x2_copy(j, di).start()

    def stage_ag1(j):
        sl = lax.rem(j, SL)
        for di in (0, 1):
            x1_copy(j, di).wait_send()
        for di in (0, 1):
            x2_copy(j, di).wait_recv()
        at = rows(r * OW, OW)
        total = PX[sl, :, at, :].astype(F32) + R2[sl, 0].astype(F32) + R2[sl, 1].astype(F32)
        gate, up, hg = total[0], total[1], total[2]
        sig = jax.nn.sigmoid(gate)
        G[sl, 0, at, :] = (gate * sig * up).astype(BF)
        G[sl, 1, at, :] = (hg * up * sig * (1.0 + gate * (1.0 - sig))).astype(BF)
        G[sl, 2, at, :] = (hg * gate * sig).astype(BF)
        for di in (0, 1):
            g1_copy(j, di, r).start()

    def stage_ag2(j):
        for di in (0, 1):
            frm = (left, right)[di]
            g1_copy(j, di, frm).wait_recv()
            g2_copy(j, di, frm).start()

    def stage_e(j):
        sl, ps = lax.rem(j, SL), lax.rem(j, PS)
        for di in (0, 1):
            x2_copy(j, di).wait_send()
            g1_copy(j, di, r).wait_send()
        for di in (0, 1):
            g2_copy(j, di, opp).wait_recv()
        hid = G[sl, 0]
        dgu = jnp.concatenate([G[sl, 1], G[sl, 2]], axis=1)
        for m in range(4):
            at = pl.ds(m * 256, 256)
            gu = jnp.dot(TT[at, :], dgu, preferred_element_type=F32)
            PZ[ps, 0, at, :] = gu[:, :CW].astype(BF)
            PZ[ps, 1, at, :] = gu[:, CW:].astype(BF)
        hid_t = hid.T
        for h in range(2):
            down = jnp.dot(hid_t, C[:, h * 512 : h * 512 + 512], preferred_element_type=F32).astype(BF)
            for ub in range(8):
                u = lax.rem(ub + 16 - lax.rem(6 * k + j, 8), 8)
                top = (2 * lax.rem(u, 4) + lax.div(u, 4)) * 128 + h * 64
                for cb in range(4):
                    tile = down[ub * ST : ub * ST + ST, cb * 128 : cb * 128 + 128]
                    PZ[ps, 2, pl.ds(pl.multiple_of(top + cb * ST, ST), ST), :] = tile
        for di in (0, 1):
            z_copy(j, di, 0).start()
        for m in range(4):
            at = pl.ds(m * 128, 128)
            ACC[at, :] += jnp.dot(G[sl, 0, at, :], WD[j], preferred_element_type=F32)

    def stage_z(s):
        def run(j):
            sl, ps = lax.rem(j, ZS), lax.rem(j, PS)
            if s == 1:
                for di in (0, 1):
                    g2_copy(j, di, (left, right)[di]).wait_send()
            else:
                for di in (0, 1):
                    z_copy(j, di, s - 2).wait_send()
            for di in (0, 1):
                z_copy(j, di, s - 1).wait_recv()
                part = PZ[ps, :, zrow(di, s), :].astype(F32)
                ZB[di, s - 1, sl] = (ZB[di, s - 1, sl].astype(F32) + part).astype(BF)
                z_copy(j, di, s).start()

        return run

    def swap_copy(j):
        return remote(XS.at[j], XR.at[j], s_xs.at[j], r_xs.at[j], depth=mate)

    def put(value, kk, j):
        lane = lax.div(lax.broadcasted_iota(jnp.int32, (2, 64, CW), 2), ST)
        for g in range(4):
            turned = pltpu.roll(value, CW - ST * g, 2) if g else value
            for zz in (2 * g, 2 * g + 1):
                at = lane_block(kk, j, zz)
                here = lane == lax.rem(4 * zz + 6 * kk + j, 8)
                OGU[:, :, at] = jnp.where(here, turned, OGU[:, :, at])

    def put_swapped(j):
        swap_copy(j).wait_recv()
        put(XR[j].astype(F32), 1 - k, j)

    def stage_fin(j):
        sl, ps = lax.rem(j, ZS), lax.rem(j, PS)
        sums = []
        for di in (0, 1):
            for s in (5, 6):
                z_copy(j, di, s).wait_send()
        for di in (0, 1):
            z_copy(j, di, 6).wait_recv()
            part = PZ[ps, :, rows(z * 128 + di * 64, 64), :].astype(F32)
            sums.append(ZB[di, 6, sl].astype(F32) + part)
        lo, hi = sums
        first = k == 0
        put(jnp.where(first, lo[:2], hi[:2]), k, j)
        XS[j] = jnp.where(first, hi[:2], lo[:2]).astype(BF)
        swap_copy(j).start()
        for h in (0, 1):
            for cb in range(4):
                tile = sums[h][2, cb * ST : cb * ST + ST].astype(BF)
                OGD[rows(j * ST, ST), h * 512 + cb * 128 : h * 512 + cb * 128 + 128] = tile

        @pl.when(j >= 2)
        def _():
            put_swapped(j - 2)

    def mate_copy():
        return remote(MS, MR, s_m.at[0], r_m.at[0], depth=mate)

    def col_copy(dy):
        return remote(MYS.at[dy], MYR.at[dy], s_my.at[dy], r_my.at[dy], col=mod(y + dy, 4))

    def mix1():
        MS[...] = ACC[rows((1 - k) * 256, 256), :].astype(BF)
        mate_copy().start()

    def mix2():
        mate_copy().wait()
        for dy in (1, 3, 2):
            yy = mod(y + dy, 4)
            total = ACC[rows(k * 256 + yy * TD, TD), :] + MR[rows(yy * TD, TD), :].astype(F32)
            MYS[dy] = total.astype(BF)
            col_copy(dy).start()

    def mix3():
        total = ACC[rows(k * 256 + y * TD, TD), :] + MR[rows(y * TD, TD), :].astype(F32)
        for dy in (1, 3, 2):
            col_copy(dy).wait()
            total = total + MYR[dy].astype(F32)
        OM[...] = total.astype(BF)
        pltpu.make_async_copy(OM, o_mix, s_out.at[0]).start()

    def transposes():
        TT[...] = T[...].T

    stages = {"A": stage_a, "RS2": stage_rs2, "AG1": stage_ag1, "AG2": stage_ag2, "E": stage_e, "FIN": stage_fin}
    for s in range(1, 7):
        stages[f"Z{s}"] = stage_z(s)
    last_e = NC - 1 + TICK["E"] // PT

    @pl.loop(0, NC + TICK["FIN"] // PT)
    def _(i):
        for parity in range(PT):
            for name in ORDER:
                if TICK[name] % PT != parity:
                    continue
                j = i - TICK[name] // PT

                @pl.when(jnp.logical_and(j >= 0, j < NC))
                def _(name=name, j=j):
                    stages[name](j)

            if parity == 0:
                pl.when(i == 0)(transposes)
            if parity == PT - 1:
                for n, step in enumerate((mix1, mix2, mix3)):
                    pl.when(i == last_e + n)(step)

    outs = []
    outs.append(pltpu.make_async_copy(OGD, o_down, s_out.at[3]))
    outs[-1].start()
    for j in (NC - 2, NC - 1):
        put_swapped(j)
    for n, o in ((0, o_gate), (1, o_up)):
        OGB[n] = OGU[n].astype(BF)
        outs.append(pltpu.make_async_copy(OGB.at[n], o, s_out.at[1 + n]))
        outs[-1].start()
    for j in range(NC):
        swap_copy(j).wait_send()
    for a in (0, 1):
        for di in range(3):
            own_copy(a, di).wait_send()
            mate_block(a, di, own).wait_send()
        for di in (0, 1):
            relay_copy(a, di, own).wait_send()
    pltpu.make_async_copy(OM, o_mix, s_out.at[0]).wait()
    for o in outs:
        o.wait()


def written(*refs):
    ins, outs, bufs, sems = refs[:4], refs[4:8], refs[8:12], refs[12]
    there = [pltpu.make_async_copy(a, b, sems.at[0, n]) for n, (a, b) in enumerate(zip(ins, bufs))]
    back = [pltpu.make_async_copy(b, o, sems.at[1, n]) for n, (b, o) in enumerate(zip(bufs, outs))]
    for c in there:
        c.start()
    for c, w in zip(there, back):
        c.wait()
        w.start()
    for w in back:
        w.wait()


def per_device(tokens, w_gate, w_up, w_down, cotangent):
    dma = pltpu.SemaphoreType.DMA
    scratch = [
        pltpu.VMEM((TK, FW), BF),
        pltpu.VMEM((TK, FW), BF),
        pltpu.VMEM((FW, TK), BF),
        pltpu.VMEM((FW, HW), BF),
        pltpu.VMEM((FW, HW), BF),
        pltpu.VMEM((FW, 2 * CW), BF),
        pltpu.VMEM((NC, CW, FW), BF),
        pltpu.VMEM((SL, 3, TK, CW), BF),
        pltpu.VMEM((SL, 2, 3, HF, CW), BF),
        pltpu.VMEM((SL, 2, 3, OW, CW), BF),
        pltpu.VMEM((SL, 3, TK, CW), BF),
        pltpu.VMEM((PS, 3, FW, CW), BF),
        pltpu.VMEM((2, 7, ZS, 3, 64, CW), BF),
        pltpu.VMEM((TK, FW), F32),
        pltpu.VMEM((NC, 2, 64, CW), BF),
        pltpu.VMEM((NC, 2, 64, CW), BF),
        pltpu.VMEM((2, 64, HW), F32),
        pltpu.VMEM((2, 64, HW), BF),
        pltpu.VMEM((HW // 16, FW), BF),
        pltpu.VMEM((256, FW), BF),
        pltpu.VMEM((256, FW), BF),
        pltpu.VMEM((4, TD, FW), BF),
        pltpu.VMEM((4, TD, FW), BF),
        pltpu.VMEM((TD, FW), BF),
        dma((2,)), dma((2,)), dma((NC,)),
        dma((2, 3)), dma((2, 8)), dma((2, 3)), dma((2, 2)), dma((2, 2)),
        dma((2, SL)), dma((2, SL)), dma((2, SL)), dma((2, SL)),
        dma((2, SL)), dma((2, SL)), dma((2, SL)), dma((2, SL)),
        dma((2, 7, ZS)), dma((2, 7, ZS)),
        dma((NC,)), dma((NC,)),
        dma((1,)), dma((1,)), dma((4,)), dma((4,)), dma((4,)),
    ]
    anyspec = pl.BlockSpec(memory_space=pl.ANY)
    out_shape = tuple(
        jax.ShapeDtypeStruct(s, BF) for s in ((TD, FW), (FW // 16, HW), (FW // 16, HW), (HW // 16, FW))
    )
    results = pl.pallas_call(
        kernel,
        out_shape=out_shape,
        in_specs=[anyspec] * 5,
        out_specs=(anyspec,) * 4,
        scratch_shapes=scratch,
        compiler_params=pltpu.CompilerParams(
            collective_id=0, has_side_effects=True, vmem_limit_bytes=58 * 1024 * 1024
        ),
    )(tokens, w_gate, w_up, w_down, cotangent)
    return pl.pallas_call(
        written,
        out_shape=out_shape,
        in_specs=[anyspec] * 4,
        out_specs=(anyspec,) * 4,
        scratch_shapes=[pltpu.VMEM(o.shape, BF) for o in out_shape] + [dma((2, 4))],
    )(*results)


def solution(mesh):
    tok, grad = P(("col", "depth"), "row"), P(("row", "depth"), "col")
    return jax.shard_map(
        per_device,
        mesh=mesh,
        in_specs=(tok, P("row", "col"), P("row", "col"), P("col", "row"), tok),
        out_specs=(tok, grad, grad, P(("col", "depth"), "row")),
        check_vma=False,
    )
```

time: 222 us -> 177 us (0.80)
  Pallas kernels: 212 us -> 176 us
  local copies, waits for them, and re-layouts: 7.01 us -> 0 us
    pallas_call x1 -> x2, Pallas kernels: 212 us -> 176 us  [the longest x1 174 us: per_device(): pl.pallas_call(kernel, out_shape=out_shape, in_specs=[anyspec] * 5, out_s...]
    unnamed x4 -> x0, local copies, waits for them, and re-layouts: 7.01 us -> none
where the time goes in v2:
time: 177 us; the launch traced here: 176 us
  Pallas kernels  176 us (99%)
    pallas_call x1, Pallas kernels, per_device(): pl.pallas_call(kernel, out_shape=out_shape, in_specs=[anyspec] * 5, out_s...  174 us

profile of v2, /device:TPU:1, one launch (start us, length us, event | category | flops | bytes accessed | tf_op | source)
XLA Modules:
  0.0 176.5 jit_solution(14146545252903292279)
XLA Ops:
  0.6 173.6 %shard_map.84 = (bf16[64,1024]{1,0:T(8,128)(2,1)}, bf16[64,3584]{1,0:T(8,128)(2,1)}, bf16[64,3584]{1,0:T(8,128)(2,1)}, bf16[224,1024]{1,0:T(8,128)(2,1)}) custom-call(bf16[64,1024]{1,0:T(8,128)(2,1)} %tok.1, bf16[1024,3584]{1,0:T(8,128)(2,1)} %wg.1, bf16[1024,3584]{1,0:T(8,128)(2,1)} %wu.1, bf16[3584,1024]{1,0:T(8,128)(2,1)} %wd.1, bf16[64,1024]{1,0:T(8,128)(2,1)} %cot.1), custom_call_target="tpu_custom_call" | custom-call | tf_op jit(solution)/shard_map/pallas_call | solution.py:435
  174.2 2.2 %shard_map.85 = (bf16[64,1024]{1,0:T(8,128)(2,1)}, bf16[64,3584]{1,0:T(8,128)(2,1)}, bf16[64,3584]{1,0:T(8,128)(2,1)}, bf16[224,1024]{1,0:T(8,128)(2,1)}) custom-call(bf16[64,1024]{1,0:T(8,128)(2,1)} %get-tuple-element.8.refs_0_, bf16[64,3584]{1,0:T(8,128)(2,1)} %get-tuple-element.9.refs_1_, bf16[64,3584]{1,0:T(8,128)(2,1)} %get-tuple-element.10.refs_2_, ...), custom_call_target="tpu_custom_call" | custom-call | tf_op jit(solution)/shard_map/pallas_call | solution.py:445

commit v3 on v2

--- a/solution.py
+++ b/solution.py
@@ -19,8 +19,8 @@
 ST = CW // NZ
 
 PT = 3
-TICK = {"A": 0, "RS2": 2, "AG1": 5, "AG2": 8, "E": 10, "Z1": 13, "Z2": 15, "Z3": 17, "Z4": 19, "Z5": 21, "Z6": 23, "FIN": 25}
-ORDER = ["FIN", "Z6", "Z5", "Z4", "Z3", "Z2", "Z1", "AG2", "AG1", "RS2", "A", "E"]
+TICK = {"A": 0, "RS2": 2, "AG1": 5, "AG2": 7, "E": 9, "Z1": 12, "Z2": 14, "Z3": 17, "FIN": 20}
+ORDER = ["FIN", "Z3", "Z2", "Z1", "AG2", "AG1", "RS2", "A", "E"]
 
 
 def remote(src, dst, ssem, rsem, **dev):
@@ -72,85 +72,15 @@
         pl.semaphore_signal(barrier, inc=1, device_id={"row": other}, device_id_type=MESH)
     for dy in range(1, 4):
         pl.semaphore_signal(barrier, inc=1, device_id={"col": mod(y + dy, 4)}, device_id_type=MESH)
-    for dd in range(1, 16):
-        pl.semaphore_signal(barrier, inc=1, device_id={"depth": mod(d + dd, 16)}, device_id_type=MESH)
+    for other in (zup, zdn, mate):
+        pl.semaphore_signal(barrier, inc=1, device_id={"depth": other}, device_id_type=MESH)
 
     for n in (0, 1):
         for q in range(4):
             wide_copy(n, q).start()
     pl.loop(0, NC)(start_down)
     ACC[...] = jnp.zeros_like(ACC)
-    pl.semaphore_wait(barrier, 20)
-
-    def block_of(a, b):
-        return (T, C)[a].at[rows(b * TD, TD), :]
-
-    yto = (mod(y + 1, 4), mod(y + 3, 4))
-    yop = 4 * k + mod(y + 2, 4)
-
-    def own_copy(a, di):
-        dev = {"depth": mate} if di == 2 else {"col": yto[di]}
-        return remote(block_of(a, own), block_of(a, own), s_ag.at[a, di], r_ag.at[a, own], **dev)
-
-    def relay_copy(a, di, b):
-        at = (T, C)[a].at[rows(b * TD + di * (TD // 2), TD // 2), :]
-        return remote(at, at, s_rl.at[a, di], r_rl.at[a, di], col=yto[di])
-
-    def mate_block(a, n, b):
-        return remote(block_of(a, b), block_of(a, b), s_fw.at[a, n], r_ag.at[a, b], depth=mate)
-
-    for a, mine in ((0, in_t), (1, in_c)):
-        mine.wait()
-        for di in range(3):
-            own_copy(a, di).start()
-    for a in (0, 1):
-        for di in (0, 1):
-            b = 4 * k + yto[1 - di]
-            mate_block(a, di, b).wait_recv()
-            relay_copy(a, di, b).start()
-            mate_block(a, di, b).start()
-    for a in (0, 1):
-        for di in (0, 1):
-            relay_copy(a, di, yop).wait_recv()
-        mate_block(a, 2, yop).start()
-    for a in (0, 1):
-        for yy in range(4):
-            mate_block(a, 0, 4 * (1 - k) + yy).wait_recv()
-
-    def xto(di):
-        return {"row": (right, left)[di]}
-
-    def x1_copy(j, di):
-        sl = lax.rem(j, SL)
-        src = PX.at[sl, :, rows(opp * OW + di * HF, HF), :]
-        return remote(src, R1.at[sl, di], s_x1.at[di, sl], r_x1.at[di, sl], **xto(di))
-
-    def x2_copy(j, di):
-        sl = lax.rem(j, SL)
-        src = PX.at[sl, :, rows((right, left)[di] * OW, OW), :]
-        return remote(src, R2.at[sl, di], s_x2.at[di, sl], r_x2.at[di, sl], **xto(di))
-
-    def g1_copy(j, di, owner):
-        sl = lax.rem(j, SL)
-        at = G.at[sl, :, rows(owner * OW, OW), :]
-        return remote(at, at, s_g1.at[di, sl], r_g1.at[di, sl], **xto(di))
-
-    def g2_copy(j, di, owner):
-        sl = lax.rem(j, SL)
-        at = G.at[sl, :, rows(owner * OW + di * HF, HF), :]
-        return remote(at, at, s_g2.at[di, sl], r_g2.at[di, sl], **xto(di))
-
-    def zrow(di, s):
-        q = mod(z - 1 - s + NZ, NZ) if di == 0 else mod(z + 1 + s, NZ)
-        return rows(q * 128 + di * 64, 64)
-
-    def z_copy(j, di, s):
-        sl = lax.rem(j, ZS)
-        if s == 0:
-            src = PZ.at[lax.rem(j, PS), :, zrow(di, 0), :]
-        else:
-            src = ZB.at[di, s - 1, sl]
-        return remote(src, ZB.at[di, s, sl], s_z.at[di, s, sl], r_z.at[di, s, sl], depth=(zup, zdn)[di])
+    pl.semaphore_wait(barrier, 8)
 
     def lane_block(kk, j, zz):
         return rows(lax.div(448 * zz + 224 * kk + ST * j, CW) * CW, CW)
@@ -160,15 +90,7 @@
         u = lax.rem(lax.div(lane, ST) + 16 - lax.rem(6 * k + j, 8), 8)
         return 2 * lax.rem(u, 4) + lax.div(u, 4)
 
-    def stage_a(j):
-        sl = lax.rem(j, SL)
-        pltpu.make_async_copy(wd.at[pl.ds(0, CW), :], WD.at[j], s_wd.at[j]).wait()
-
-        @pl.when(j == 0)
-        def _():
-            for n, (w, buf) in enumerate(((wg, WG), (wu, WU))):
-                pltpu.make_async_copy(w, buf, s_w.at[n]).wait()
-
+    def chunk_weights(j):
         which = strip_at(j)
         for n, buf in enumerate((WG, WU)):
             for q in range(8):
@@ -179,10 +101,88 @@
                     if zz // 2:
                         part = pltpu.roll(part, ST * (zz // 2), 1)
                     got = jnp.where(which == zz, part, got)
-                WC[at, n * CW : (n + 1) * CW] = got
+                WC[lax.rem(j, 2), at, n * CW : (n + 1) * CW] = got
+
+    def block_of(a, b):
+        return (T, C)[a].at[rows(b * TD, TD), :]
+
+    yto = (mod(y + 1, 4), mod(y + 3, 4))
+    yop = 4 * k + mod(y + 2, 4)
+
+    def own_copy(a, di):
+        dev = {"depth": mate} if di == 2 else {"col": yto[di]}
+        return remote(block_of(a, own), block_of(a, own), s_ag.at[a, di], r_ag.at[a, own], **dev)
+
+    def relay_copy(a, di, b):
+        at = (T, C)[a].at[rows(b * TD + di * (TD // 2), TD // 2), :]
+        return remote(at, at, s_rl.at[a, di], r_rl.at[a, di], col=yto[di])
+
+    def mate_block(a, n, b):
+        return remote(block_of(a, b), block_of(a, b), s_fw.at[a, n], r_ag.at[a, b], depth=mate)
+
+    for a, mine in ((0, in_t), (1, in_c)):
+        mine.wait()
+        for di in range(3):
+            own_copy(a, di).start()
+    for a in (0, 1):
+        for di in (0, 1):
+            b = 4 * k + yto[1 - di]
+            mate_block(a, di, b).wait_recv()
+            relay_copy(a, di, b).start()
+            mate_block(a, di, b).start()
+    for a in (0, 1):
+        for di in (0, 1):
+            relay_copy(a, di, yop).wait_recv()
+        mate_block(a, 2, yop).start()
+    for n, (w, buf) in enumerate(((wg, WG), (wu, WU))):
+        pltpu.make_async_copy(w, buf, s_w.at[n]).wait()
+    chunk_weights(0)
+    for a in (0, 1):
+        for yy in range(4):
+            mate_block(a, 0, 4 * (1 - k) + yy).wait_recv()
+
+    def xto(di):
+        return {"row": (right, left)[di]}
+
+    def x1_copy(j, di):
+        sl = lax.rem(j, SL)
+        src = PX.at[sl, :, rows(opp * OW + di * HF, HF), :]
+        return remote(src, R1.at[sl, di], s_x1.at[di, sl], r_x1.at[di, sl], **xto(di))
+
+    def x2_copy(j, di):
+        sl = lax.rem(j, SL)
+        src = PX.at[sl, :, rows((right, left)[di] * OW, OW), :]
+        return remote(src, R2.at[sl, di], s_x2.at[di, sl], r_x2.at[di, sl], **xto(di))
+
+    def g1_copy(j, di, owner):
+        sl = lax.rem(j, SL)
+        at = G.at[sl, :, rows(owner * OW, OW), :]
+        return remote(at, at, s_g1.at[di, sl], r_g1.at[di, sl], **xto(di))
+
+    def g2_copy(j, di, owner):
+        sl = lax.rem(j, SL)
+        at = G.at[sl, :, rows(owner * OW + di * HF, HF), :]
+        return remote(at, at, s_g2.at[di, sl], r_g2.at[di, sl], **xto(di))
+
+    def zblock(di, s):
+        return (mod(z + 4 - s, NZ) if di == 0 else mod(z + 4 + s, NZ)) * 128
+
+    def z_copy(j, di, s):
+        sl = lax.rem(j, ZS)
+        if s == 0:
+            half = pl.ds(di * 64, 64)
+            src = PZ.at[lax.rem(j, PS), :, rows(zblock(di, 0) + di * 64, 64), :]
+            dst = ZB.at[di, 0, sl, :, half, :]
+        else:
+            src, dst = ZB.at[di, s - 1, sl], ZB.at[di, s, sl]
+        return remote(src, dst, s_z.at[di, s, sl], r_z.at[di, s, sl], depth=(zup, zdn)[di])
+
+    def stage_a(j):
+        sl = lax.rem(j, SL)
+        pltpu.make_async_copy(wd.at[pl.ds(0, CW), :], WD.at[j], s_wd.at[j]).wait()
         for m in range(2):
             at = pl.ds(m * 256, 256)
-            gu = jnp.dot(T[at, :], WC[...], preferred_element_type=F32)
+            gu = jnp.dot(T[at, :], WC[lax.rem(j, 2)], preferred_element_type=F32)
             h = lax.dot_general(C[at, :], WD[j], (((1,), (1,)), ((), ())), preferred_element_type=F32)
             PX[sl, 0, at, :] = gu[:, :CW].astype(BF)
             PX[sl, 1, at, :] = gu[:, CW:].astype(BF)
@@ -260,8 +260,12 @@
                     z_copy(j, di, s - 2).wait_send()
             for di in (0, 1):
                 z_copy(j, di, s - 1).wait_recv()
-                part = PZ[ps, :, zrow(di, s), :].astype(F32)
-                ZB[di, s - 1, sl] = (ZB[di, s - 1, sl].astype(F32) + part).astype(BF)
+                for h in (0, 1):
+                    at = pl.ds(h * 64, 64)
+                    part = PZ[ps, :, rows(zblock(di, s) + h * 64, 64), :]
+                    if s > 1 or h == di:
+                        part = (part.astype(F32) + ZB[di, s - 1, sl, :, at, :].astype(F32)).astype(BF)
+                    ZB[di, s - 1, sl, :, at, :] = part
                 z_copy(j, di, s).start()
 
         return run
@@ -286,12 +290,14 @@
         sl, ps = lax.rem(j, ZS), lax.rem(j, PS)
         sums = []
         for di in (0, 1):
-            for s in (5, 6):
+            for s in (2, 3):
                 z_copy(j, di, s).wait_send()
         for di in (0, 1):
-            z_copy(j, di, 6).wait_recv()
-            part = PZ[ps, :, rows(z * 128 + di * 64, 64), :].astype(F32)
-            sums.append(ZB[di, 6, sl].astype(F32) + part)
+            z_copy(j, di, 3).wait_recv()
+        for h in (0, 1):
+            at = pl.ds(h * 64, 64)
+            part = PZ[ps, :, rows(z * 128 + h * 64, 64), :].astype(F32)
+            sums.append(part + ZB[0, 3, sl, :, at, :].astype(F32) + ZB[1, 3, sl, :, at, :].astype(F32))
         lo, hi = sums
         first = k == 0
         put(jnp.where(first, lo[:2], hi[:2]), k, j)
@@ -336,7 +342,7 @@
         TT[...] = T[...].T
 
     stages = {"A": stage_a, "RS2": stage_rs2, "AG1": stage_ag1, "AG2": stage_ag2, "E": stage_e, "FIN": stage_fin}
-    for s in range(1, 7):
+    for s in range(1, 4):
         stages[f"Z{s}"] = stage_z(s)
     last_e = NC - 1 + TICK["E"] // PT
 
@@ -355,6 +361,7 @@
             if parity == 0:
                 pl.when(i == 0)(transposes)
             if parity == PT - 1:
+                pl.when(i < NC - 1)(lambda: chunk_weights(i + 1))
                 for n, step in enumerate((mix1, mix2, mix3)):
                     pl.when(i == last_e + n)(step)
 
@@ -401,14 +408,14 @@
         pltpu.VMEM((FW, TK), BF),
         pltpu.VMEM((FW, HW), BF),
         pltpu.VMEM((FW, HW), BF),
-        pltpu.VMEM((FW, 2 * CW), BF),
+        pltpu.VMEM((2, FW, 2 * CW), BF),
         pltpu.VMEM((NC, CW, FW), BF),
         pltpu.VMEM((SL, 3, TK, CW), BF),
         pltpu.VMEM((SL, 2, 3, HF, CW), BF),
         pltpu.VMEM((SL, 2, 3, OW, CW), BF),
         pltpu.VMEM((SL, 3, TK, CW), BF),
         pltpu.VMEM((PS, 3, FW, CW), BF),
-        pltpu.VMEM((2, 7, ZS, 3, 64, CW), BF),
+        pltpu.VMEM((2, 4, ZS, 3, 128, CW), BF),
         pltpu.VMEM((TK, FW), F32),
         pltpu.VMEM((NC, 2, 64, CW), BF),
         pltpu.VMEM((NC, 2, 64, CW), BF),
@@ -424,7 +431,7 @@
         dma((2, 3)), dma((2, 8)), dma((2, 3)), dma((2, 2)), dma((2, 2)),
         dma((2, SL)), dma((2, SL)), dma((2, SL)), dma((2, SL)),
         dma((2, SL)), dma((2, SL)), dma((2, SL)), dma((2, SL)),
-        dma((2, 7, ZS)), dma((2, 7, ZS)),
+        dma((2, 4, ZS)), dma((2, 4, ZS)),
         dma((NC,)), dma((NC,)),
         dma((1,)), dma((1,)), dma((4,)), dma((4,)), dma((4,)),
     ]

time: 177 us -> 163 us (0.921)
  Pallas kernels: 176 us -> 162 us
    pallas_call x1, Pallas kernels: 174 us -> 160 us  [per_device(): pl.pallas_call(kernel, out_shape=out_shape, in_specs=[anyspec] * 5, out_s...]
where the time goes in v3:
time: 163 us
  Pallas kernels  162 us (99%)
    pallas_call x1, Pallas kernels, per_device(): pl.pallas_call(kernel, out_shape=out_shape, in_specs=[anyspec] * 5, out_s...  160 us

profile of v3, /device:TPU:1, one launch (start us, length us, event | category | flops | bytes accessed | tf_op | source)
XLA Modules:
  0.0 162.8 jit_solution(16560321778061749248)
XLA Ops:
  0.6 160.0 %shard_map.84 = (bf16[64,1024]{1,0:T(8,128)(2,1)}, bf16[64,3584]{1,0:T(8,128)(2,1)}, bf16[64,3584]{1,0:T(8,128)(2,1)}, bf16[224,1024]{1,0:T(8,128)(2,1)}) custom-call(bf16[64,1024]{1,0:T(8,128)(2,1)} %tok.1, bf16[1024,3584]{1,0:T(8,128)(2,1)} %wg.1, bf16[1024,3584]{1,0:T(8,128)(2,1)} %wu.1, bf16[3584,1024]{1,0:T(8,128)(2,1)} %wd.1, bf16[64,1024]{1,0:T(8,128)(2,1)} %cot.1), custom_call_target="tpu_custom_call" | custom-call | tf_op jit(solution)/shard_map/pallas_call | solution.py:442
  160.6 2.2 %shard_map.85 = (bf16[64,1024]{1,0:T(8,128)(2,1)}, bf16[64,3584]{1,0:T(8,128)(2,1)}, bf16[64,3584]{1,0:T(8,128)(2,1)}, bf16[224,1024]{1,0:T(8,128)(2,1)}) custom-call(bf16[64,1024]{1,0:T(8,128)(2,1)} %get-tuple-element.8.refs_0_, bf16[64,3584]{1,0:T(8,128)(2,1)} %get-tuple-element.9.refs_1_, bf16[64,3584]{1,0:T(8,128)(2,1)} %get-tuple-element.10.refs_2_, ...), custom_call_target="tpu_custom_call" | custom-call | tf_op jit(solution)/shard_map/pallas_call | solution.py:452

commit v4 on v3

--- a/solution.py
+++ b/solution.py
@@ -19,7 +19,7 @@
 ST = CW // NZ
 
 PT = 3
-TICK = {"A": 0, "RS2": 2, "AG1": 5, "AG2": 7, "E": 9, "Z1": 12, "Z2": 14, "Z3": 17, "FIN": 20}
+TICK = {"A": 0, "RS2": 2, "AG1": 5, "AG2": 8, "E": 10, "Z1": 13, "Z2": 16, "Z3": 19, "FIN": 22}
 ORDER = ["FIN", "Z3", "Z2", "Z1", "AG2", "AG1", "RS2", "A", "E"]
 
 

time: 163 us -> 166 us (1.018)
  Pallas kernels: 162 us -> 165 us
    pallas_call x1, Pallas kernels: 160 us -> 163 us  [per_device(): pl.pallas_call(kernel, out_shape=out_shape, in_specs=[anyspec] * 5, out_s...]
where the time goes in v4:
time: 166 us
  Pallas kernels  165 us (99%)
    pallas_call x1, Pallas kernels, per_device(): pl.pallas_call(kernel, out_shape=out_shape, in_specs=[anyspec] * 5, out_s...  163 us

profile of v4, /device:TPU:1, one launch (start us, length us, event | category | flops | bytes accessed | tf_op | source)
XLA Modules:
  0.0 165.7 jit_solution(11839820266966522415)
XLA Ops:
  0.6 162.8 %shard_map.84 = (bf16[64,1024]{1,0:T(8,128)(2,1)}, bf16[64,3584]{1,0:T(8,128)(2,1)}, bf16[64,3584]{1,0:T(8,128)(2,1)}, bf16[224,1024]{1,0:T(8,128)(2,1)}) custom-call(bf16[64,1024]{1,0:T(8,128)(2,1)} %tok.1, bf16[1024,3584]{1,0:T(8,128)(2,1)} %wg.1, bf16[1024,3584]{1,0:T(8,128)(2,1)} %wu.1, bf16[3584,1024]{1,0:T(8,128)(2,1)} %wd.1, bf16[64,1024]{1,0:T(8,128)(2,1)} %cot.1), custom_call_target="tpu_custom_call" | custom-call | tf_op jit(solution)/shard_map/pallas_call | solution.py:442
  163.5 2.2 %shard_map.85 = (bf16[64,1024]{1,0:T(8,128)(2,1)}, bf16[64,3584]{1,0:T(8,128)(2,1)}, bf16[64,3584]{1,0:T(8,128)(2,1)}, bf16[224,1024]{1,0:T(8,128)(2,1)}) custom-call(bf16[64,1024]{1,0:T(8,128)(2,1)} %get-tuple-element.8.refs_0_, bf16[64,3584]{1,0:T(8,128)(2,1)} %get-tuple-element.9.refs_1_, bf16[64,3584]{1,0:T(8,128)(2,1)} %get-tuple-element.10.refs_2_, ...), custom_call_target="tpu_custom_call" | custom-call | tf_op jit(solution)/shard_map/pallas_call | solution.py:452
